TPU v7x, 32 devices: a whole 2x2x4 slice. The times are simulated.
32 devices in a mesh: grp: 2 (over x), seq: 16 (over z, y, core).
Axes of the slice: x: 2, y: 2, z: 4, core: 2. Of those that a mesh axis runs over, the one named last changes fastest.
Arguments:
- queries: bfloat16 [8192, 32, 128], P(('grp', 'seq')), parts along dimension 0, may hold values from -45 to 45
- keys: bfloat16 [8192, 8, 128], P(('grp', 'seq')), parts along dimension 0, may hold values from -6 to 6
- values: bfloat16 [8192, 8, 128], P(('grp', 'seq')), parts along dimension 0, may hold values from -6 to 6
- global_ids: int32 [8], P('grp'), parts along dimension 0, may hold values from 0 to 31, as said below
- doc_lengths: int32 [32], P('grp'), parts along dimension 0, may hold values from 1 to 1024, 4096 in all
Outputs:
- attended: bfloat16 [8192, 32, 128], P(('grp', 'seq')), parts along dimension 0
There are 2 independent parts, one for each index of `grp`. A program takes and returns all parts, laid end to end along the dimension named above; each array names one. Nothing has to cross between parts.
Inputs may be any that keep to these rules, and one draw needn't show every extreme that they name: `global_ids`: 4 distinct block numbers.
All inputs are finite; a program needn't handle non-finite values.
Results may differ from a plain program's by a relative error of at most 0.0065.
Values may be sent and summed in bfloat16 or wider, within the bound.
A program may use at most 64 MiB of HBM per device.

v0:
```python
import math

import jax
import jax.numpy as jnp
from jax import lax
from jax.sharding import PartitionSpec as P

BLK = 128
WIN = 3


masked_score = -1e30


def shifted(shard, axis, by):
    length = lax.axis_size(axis)
    pairs = [(i, i + by) for i in range(length) if 0 <= i + by < length]
    return lax.ppermute(shard, axis, pairs)


def doc_index(positions, doc_ends):
    return jnp.sum((positions[:, None] >= doc_ends[None, :]).astype(jnp.int32), axis=1)


def per_device(queries, keys, values, global_ids, doc_lengths):
    tok_rows = queries.shape[0]
    heads_here = queries.shape[1]
    head_size = queries.shape[2]
    kv_count = keys.shape[1]
    group_size = heads_here // kv_count
    blocks_here = tok_rows // BLK
    score_scale = 1.0 / math.sqrt(head_size)
    device_rank = lax.axis_index("seq")
    first_pos = device_rank * tok_rows
    doc_ends = jnp.cumsum(doc_lengths)
    offsets = jnp.arange(BLK, dtype=jnp.int32)
    query_pos = first_pos + jnp.arange(tok_rows, dtype=jnp.int32)
    query_doc = doc_index(query_pos, doc_ends)
    query_block = query_pos // BLK
    grouped = queries.reshape(tok_rows, kv_count, group_size, head_size)

    def update(running, key_block, value_block, key_pos, extra_ok, bounded):
        if bounded:
            key_doc = doc_index(key_pos, doc_ends)
            allowed = (
                (key_pos[None, :] <= query_pos[:, None])
                & (key_doc[None, :] == query_doc[:, None])
                & extra_ok
            )
        else:
            allowed = extra_ok
        mask_wide = allowed[:, None, None, :]

        def compute(carried):
            row_peak, denom_sum, weighted = carried
            scores = (
                jnp.einsum("qkgd,tkd->qkgt", grouped, key_block, preferred_element_type=jnp.float32)
                * score_scale
            )
            scores = jnp.where(mask_wide, scores, masked_score)
            new_peak = jnp.maximum(row_peak, jnp.max(scores, axis=-1))
            exp_terms = jnp.where(mask_wide, jnp.exp(scores - new_peak[..., None]), 0.0)
            factor = jnp.exp(row_peak - new_peak)
            denom_sum = denom_sum * factor + jnp.sum(exp_terms, axis=-1)
            weighted = weighted * factor[..., None] + jnp.einsum(
                "qkgt,tkd->qkgd",
                exp_terms.astype(jnp.bfloat16),
                value_block,
                preferred_element_type=jnp.float32,
            )
            return (new_peak, denom_sum, weighted)

        return lax.cond(jnp.any(allowed), compute, lambda carried: carried, running)

    running = (
        jnp.full((tok_rows, kv_count, group_size), masked_score, jnp.float32),
        jnp.zeros((tok_rows, kv_count, group_size), jnp.float32),
        jnp.zeros((tok_rows, kv_count, group_size, head_size), jnp.float32),
    )
    earlier = shifted((keys, values), "seq", 1)
    near_keys = jnp.concatenate([earlier[0], keys], axis=0)
    near_vals = jnp.concatenate([earlier[1], values], axis=0)

    def window_turn(column, running):
        key_pos = first_pos - tok_rows + column * BLK + offsets
        extra_ok = (key_pos >= 0)[None, :] & (
            query_block[:, None] - (key_pos // BLK)[None, :] < WIN
        )
        key_block = lax.dynamic_slice_in_dim(near_keys, column * BLK, BLK, 0)
        value_block = lax.dynamic_slice_in_dim(near_vals, column * BLK, BLK, 0)
        return update(running, key_block, value_block, key_pos, extra_ok, True)

    running = lax.fori_loop(0, 2 * blocks_here, window_turn, running)

    def global_step(block_id, key_block, value_block, running):
        key_pos = block_id * BLK + offsets
        block_gap = query_block - block_id
        inside = (block_gap >= 0) & (block_gap < WIN)
        extra_ok = jnp.broadcast_to(jnp.logical_not(inside)[:, None], (tok_rows, BLK))
        return update(running, key_block, value_block, key_pos, extra_ok, False)

    global_count = global_ids.shape[0]
    owned_here = global_ids // blocks_here == device_rank
    local_slots = global_ids % blocks_here
    key_cube = keys.reshape(blocks_here, BLK, kv_count, head_size)[local_slots]
    val_cube = values.reshape(blocks_here, BLK, kv_count, head_size)[local_slots]
    lowest = jnp.array(-jnp.inf, jnp.bfloat16)
    key_cube = jnp.where(owned_here[:, None, None, None], key_cube, lowest)
    val_cube = jnp.where(owned_here[:, None, None, None], val_cube, lowest)
    key_cube, val_cube = lax.pmax((key_cube, val_cube), "seq")

    def batch_turn(step_index, running):
        return global_step(
            global_ids[step_index], key_cube[step_index], val_cube[step_index], running
        )

    running = lax.fori_loop(0, global_count, batch_turn, running)
    row_peak, denom_sum, weighted = running
    attended = weighted / denom_sum[..., None]
    return attended.astype(jnp.bfloat16).reshape(tok_rows, heads_here, head_size)


def solution(mesh):
    in_specs = (
        P(("grp", "seq"), None, None),
        P(("grp", "seq"), None, None),
        P(("grp", "seq"), None, None),
        P("grp"),
        P("grp"),
    )
    out_specs = P(("grp", "seq"), None, None)
    return jax.shard_map(
        per_device, mesh=mesh, in_specs=in_specs, out_specs=out_specs, check_vma=False
    )
```

profile of v0, /device:TPU:0, one launch (start us, length us, event | category | flops | bytes accessed | tf_op | source)
XLA Modules:
  0.0 183.6 jit_solution(17382248250824928166)
XLA Ops:
  6.5 2.0 %copy.29 = bf16[256,8,128]{2,0,1:T(8,128)(2,1)} copy(bf16[256,8,128]{2,1,0:T(8,128)(2,1)} %param.14) | data formatting | bytes 1048576 | tf_op args[1]
  8.5 3.2 %collective-permute-start = (bf16[256,8,128]{2,0,1:T(8,128)(2,1)}, bf16[256,8,128]{2,0,1:T(8,128)(2,1)}, u32[]{:S(2)}, u32[]{:S(2)}) collective-permute-start(bf16[256,8,128]{2,0,1:T(8,128)(2,1)} %copy.29), channel_id=1, source_target_pairs={{0,1},{1,2},{2,3},{3,4},{4,5},{5,6},{6,7},{7,8},{8,9},{9,10},{10,1... | collective-permute-start | bytes 1572872 | tf_op jit(solution)/shard_map/ppermute | solution.py:18
  11.7 1.9 %copy.32 = bf16[256,8,128]{2,0,1:T(8,128)(2,1)} copy(bf16[256,8,128]{2,1,0:T(8,128)(2,1)} %param.15) | data formatting | bytes 1048576 | tf_op args[2]
  13.6 4.5 %collective-permute-start.1 = (bf16[256,8,128]{2,0,1:T(8,128)(2,1)}, bf16[256,8,128]{2,0,1:T(8,128)(2,1)}, u32[]{:S(2)}, u32[]{:S(2)}) collective-permute-start(bf16[256,8,128]{2,0,1:T(8,128)(2,1)} %copy.32), channel_id=1, source_target_pairs={{0,1},{1,2},{2,3},{3,4},{4,5},{5,6},{6,7},{7,8},{8,9},{9,10},{10,1... | collective-permute-start | bytes 1572872 | tf_op jit(solution)/shard_map/ppermute | solution.py:18
  19.5 1.8 gather_fusion.1
  22.1 1.6 broadcast_select_fusion
  24.0 2.4 %copy.31 = bf16[256,32,128]{2,0,1:T(8,128)(2,1)S(1)} copy(bf16[256,32,128]{2,1,0:T(8,128)(2,1)} %param.13) | data formatting | bytes 4194304 | tf_op args[0]
  26.5 2.2 %pad_maximum_fusion = bf16[512,8,128]{2,0,1:T(8,128)(2,1)} fusion(bf16[256,8,128]{2,0,1:T(8,128)(2,1)} %copy.29, bf16[256,8,128]{2,0,1:T(8,128)(2,1)} %collective-permute-done), kind=kLoop, calls=%fused_computation.83 | loop fusion | flops 2097152 | bytes 2097152 | tf_op jit(solution)/shard_map/concatenate | solution.py:81
  28.7 1.3 pad_maximum_fusion.1
  30.0 2.4 %broadcast_in_dim.152 = f32[256,8,4,128]{3,0,2,1:T(8,128)} broadcast(f32[]{:T(128)} %constant.240.clone.1), dimensions={} | broadcast | bytes 4194308 | tf_op jit(solution)/shard_map/broadcast_in_dim | solution.py:78
  32.5 24.8 %while.40 = (s32[]{:T(128)}, f32[256,8,4]{0,2,1:T(4,128)S(1)}, f32[256,8,4]{0,2,1:T(4,128)S(1)}, f32[256,8,4,128]{3,0,2,1:T(8,128)}, s32[]{:T(128)}, /*index=5*/...) while((s32[]{:T(128)}, f32[256,8,4]{0,2,1:T(4,128)S(1)}, ...), condition=%wide.region_9.10_spmd.clone.clone, body=%wide.region_2.9_spmd.clone.clone.sunk | while | flops 553119872 | bytes 57816952 | solution.py:93
  32.6 0.9 fusion.60
  34.3 0.9 fusion.60
  35.9 0.9 fusion.60
  37.4 9.1 %conditional.8 = ((f32[256,8,4]{0,2,1:T(4,128)S(1)}, f32[256,8,4]{0,2,1:T(4,128)S(1)}, f32[256,8,4,128]{3,0,2,1:T(8,128)})) conditional(s32[]{:T(128)} %convert_element_type.63, (f32[256,8,4]{0,2,1:T(4,128)S(1)}, f32[256,8,4]{0,2,1:T(4,128)S(1)}, f32[256,8,4,128]{3,0,2,1:T(8,128)}) %tuple.122, (s32[128]{0:T(128)S(1)}, s32[256]{0:T(256)S(1)}, ...), branch_computations={%region_5.5_spmd, %region_6.8_spmd} | conditional | flops 552845312 | bytes 57807620 | solution.py:73
  37.6 1.9 %fusion.8 = (f32[256,8,4]{0,2,1:T(4,128)S(1)}, f32[8,128,256,4]{2,1,3,0:T(8,128)S(1)}) fusion(pred[256,128]{0,1:T(8,128)(4,1)S(1)} %fusion.23, bf16[256,8,4,128]{3,0,2,1:T(8,128)(2,1)S(1)} %get-tuple-element.725, bf16[512,8,128]{2,0,1:T(8,128)(2,1)} %get-tuple-element.723, s32[]{:T(128)S(6)} %select_n.77), kind=kOutput, calls=%fused_computation.9 | convolution fusion | flops 271572992 | bytes 6619140 | tf_op jit(solution)/shard_map/while/body/eval_jaxpr/cond/branch_1_fun/qkgd,tkd->qkgt/dot_general | solution.py:57
  39.5 1.1 fusion.10
  40.7 3.9 %bitcast_add_fusion = f32[256,8,4,128]{3,0,2,1:T(8,128)S(1)} fusion(f32[256,8,4,128]{3,0,2,1:T(8,128)S(1)} %copy-done, f32[8,128,256,4]{2,1,3,0:T(8,128)S(1)} %get-tuple-element.930, f32[256,8,4]{0,2,1:T(4,128)S(1)} %bitcast.86, f32[256,8,4]{0,2,1:T(4,128)S(1)} %max.13, pred[256,128]{0,1:T(8,128)(4,1)S(1)} %fusion.23, ...), kind=kOutput, calls=%fused_computation.6 | convolution fusion | flops 275775488 | bytes 12943364 | tf_op jit(solution)/shard_map/while/body/eval_jaxpr/cond/branch_1_fun/qkgt,tkd->qkgd/dot_general | solution.py:65
  44.6 1.9 %copy-done.1 = f32[256,8,4,128]{3,0,2,1:T(8,128)} copy-done((f32[256,8,4,128]{3,0,2,1:T(8,128)}, f32[256,8,4,128]{3,0,2,1:T(8,128)S(1)}, u32[]{:S(2)}) %copy-start.1) | copy-done | bytes 4194328 | tf_op jit(solution)/shard_map/while/body/eval_jaxpr/cond
  46.7 0.9 fusion.60
  48.2 9.1 %conditional.8 = ((f32[256,8,4]{0,2,1:T(4,128)S(1)}, f32[256,8,4]{0,2,1:T(4,128)S(1)}, f32[256,8,4,128]{3,0,2,1:T(8,128)})) conditional(s32[]{:T(128)} %convert_element_type.63, (f32[256,8,4]{0,2,1:T(4,128)S(1)}, f32[256,8,4]{0,2,1:T(4,128)S(1)}, f32[256,8,4,128]{3,0,2,1:T(8,128)}) %tuple.122, (s32[128]{0:T(128)S(1)}, s32[256]{0:T(256)S(1)}, ...), branch_computations={%region_5.5_spmd, %region_6.8_spmd} | conditional | flops 552845312 | bytes 57807620 | solution.py:73
  48.3 1.9 %fusion.8 = (f32[256,8,4]{0,2,1:T(4,128)S(1)}, f32[8,128,256,4]{2,1,3,0:T(8,128)S(1)}) fusion(pred[256,128]{0,1:T(8,128)(4,1)S(1)} %fusion.23, bf16[256,8,4,128]{3,0,2,1:T(8,128)(2,1)S(1)} %get-tuple-element.725, bf16[512,8,128]{2,0,1:T(8,128)(2,1)} %get-tuple-element.723, s32[]{:T(128)S(6)} %select_n.77), kind=kOutput, calls=%fused_computation.9 | convolution fusion | flops 271572992 | bytes 6619140 | tf_op jit(solution)/shard_map/while/body/eval_jaxpr/cond/branch_1_fun/qkgd,tkd->qkgt/dot_general | solution.py:57
  50.3 1.1 fusion.10
  51.4 3.9 %bitcast_add_fusion = f32[256,8,4,128]{3,0,2,1:T(8,128)S(1)} fusion(f32[256,8,4,128]{3,0,2,1:T(8,128)S(1)} %copy-done, f32[8,128,256,4]{2,1,3,0:T(8,128)S(1)} %get-tuple-element.930, f32[256,8,4]{0,2,1:T(4,128)S(1)} %bitcast.86, f32[256,8,4]{0,2,1:T(4,128)S(1)} %max.13, pred[256,128]{0,1:T(8,128)(4,1)S(1)} %fusion.23, ...), kind=kOutput, calls=%fused_computation.6 | convolution fusion | flops 275775488 | bytes 12943364 | tf_op jit(solution)/shard_map/while/body/eval_jaxpr/cond/branch_1_fun/qkgt,tkd->qkgd/dot_general | solution.py:65
  55.4 1.9 %copy-done.1 = f32[256,8,4,128]{3,0,2,1:T(8,128)} copy-done((f32[256,8,4,128]{3,0,2,1:T(8,128)}, f32[256,8,4,128]{3,0,2,1:T(8,128)S(1)}, u32[]{:S(2)}) %copy-start.1) | copy-done | bytes 4194328 | tf_op jit(solution)/shard_map/while/body/eval_jaxpr/cond
  57.3 64.8 %all-reduce.3.cloned.1.call-done = (bf16[4,128,8,128]{3,2,1,0:T(8,128)(2,1)}, bf16[4,128,8,128]{3,2,1,0:T(8,128)(2,1)}) async-done(((bf16[4,128,8,128]{3,2,1,0:T(8,128)(2,1)}, bf16[4,128,8,128]{3,2,1,0:T(8,128)(2,1)}), (bf16[4,128,8,128]{3,2,1,0:T(8,128)(2,1)}, bf16[4,128,8,128]{3,2,1,0:T(8,128)(2,1)})) %all-reduce.3.cloned.1.call-update) | async-done | bytes 2097168 | tf_op jit(solution)/shard_map/pmax | solution.py:110
  122.1 1.5 copy.34
  123.6 2.4 %copy.35 = bf16[4,128,8,128]{3,1,2,0:T(8,128)(2,1)} copy(bf16[4,128,8,128]{3,2,1,0:T(8,128)(2,1)} %get-tuple-element.924) | data formatting | bytes 2097152
  126.0 45.0 %while.39 = (s32[]{:T(128)}, f32[256,8,4]{0,2,1:T(4,128)S(1)}, f32[256,8,4]{0,2,1:T(4,128)S(1)}, f32[256,8,4,128]{3,0,2,1:T(8,128)}, s32[4]{0:T(128)S(1)}, /*ind...) while((s32[]{:T(128)}, f32[256,8,4]{0,2,1:T(4,128)S(1)}, ...), condition=%wide.region_18.19_spmd.clone, body=%wide.region_12.18_spmd.clone.sunk | while | flops 552659456 | bytes 57677120 | solution.py:117
  129.4 7.9 %conditional.7 = ((f32[256,8,4]{0,2,1:T(4,128)S(1)}, f32[256,8,4]{0,2,1:T(4,128)S(1)}, f32[256,8,4,128]{3,0,2,1:T(8,128)})) conditional(s32[]{:T(128)} %convert_element_type.61, (f32[256,8,4]{0,2,1:T(4,128)S(1)}, f32[256,8,4]{0,2,1:T(4,128)S(1)}, f32[256,8,4,128]{3,0,2,1:T(8,128)}) %tuple.117, (s32[256]{0:T(256)S(1)}, ...), branch_computations={%region_14.14_spmd, %region_15.17_spmd} | conditional | flops 552616960 | bytes 57675356 | solution.py:73
  129.5 0.8 bitcast_reduce_fusion
  130.3 1.1 fusion.32
  131.6 3.7 %bitcast_add_fusion.1 = f32[256,8,4,128]{3,0,2,1:T(8,128)S(1)} fusion(f32[256,8,4,128]{3,0,2,1:T(8,128)S(1)} %copy-done.2, f32[8,128,256,4]{2,1,3,0:T(8,128)S(1)} %get-tuple-element.936, f32[256,8,4]{0,2,1:T(4,128)S(1)} %bitcast.87, f32[256,8,4]{0,2,1:T(4,128)S(1)} %max.14, pred[256]{0:T(512)(128)(4,1)S(1)} %and_not_fusion, ...), kind=kOutput, calls=%fused_computation.32 | convolution fusion | flops 275775488 | bytes 12912128 | tf_op jit(solution)/shard_map/while/body/eval_jaxpr/cond/branch_1_fun/qkgt,tkd->qkgd/dot_general | solution.py:65
  135.4 1.9 %copy-done.3 = f32[256,8,4,128]{3,0,2,1:T(8,128)} copy-done((f32[256,8,4,128]{3,0,2,1:T(8,128)}, f32[256,8,4,128]{3,0,2,1:T(8,128)S(1)}, u32[]{:S(2)}) %copy-start.3) | copy-done | bytes 4194328 | tf_op jit(solution)/shard_map/while/body/eval_jaxpr/cond
  140.7 7.9 %conditional.7 = ((f32[256,8,4]{0,2,1:T(4,128)S(1)}, f32[256,8,4]{0,2,1:T(4,128)S(1)}, f32[256,8,4,128]{3,0,2,1:T(8,128)})) conditional(s32[]{:T(128)} %convert_element_type.61, (f32[256,8,4]{0,2,1:T(4,128)S(1)}, f32[256,8,4]{0,2,1:T(4,128)S(1)}, f32[256,8,4,128]{3,0,2,1:T(8,128)}) %tuple.117, (s32[256]{0:T(256)S(1)}, ...), branch_computations={%region_14.14_spmd, %region_15.17_spmd} | conditional | flops 552616960 | bytes 57675356 | solution.py:73
  141.5 1.1 fusion.32
  142.9 3.7 %bitcast_add_fusion.1 = f32[256,8,4,128]{3,0,2,1:T(8,128)S(1)} fusion(f32[256,8,4,128]{3,0,2,1:T(8,128)S(1)} %copy-done.2, f32[8,128,256,4]{2,1,3,0:T(8,128)S(1)} %get-tuple-element.936, f32[256,8,4]{0,2,1:T(4,128)S(1)} %bitcast.87, f32[256,8,4]{0,2,1:T(4,128)S(1)} %max.14, pred[256]{0:T(512)(128)(4,1)S(1)} %and_not_fusion, ...), kind=kOutput, calls=%fused_computation.32 | convolution fusion | flops 275775488 | bytes 12912128 | tf_op jit(solution)/shard_map/while/body/eval_jaxpr/cond/branch_1_fun/qkgt,tkd->qkgd/dot_general | solution.py:65
  146.6 1.9 %copy-done.3 = f32[256,8,4,128]{3,0,2,1:T(8,128)} copy-done((f32[256,8,4,128]{3,0,2,1:T(8,128)}, f32[256,8,4,128]{3,0,2,1:T(8,128)S(1)}, u32[]{:S(2)}) %copy-start.3) | copy-done | bytes 4194328 | tf_op jit(solution)/shard_map/while/body/eval_jaxpr/cond
  151.9 7.9 %conditional.7 = ((f32[256,8,4]{0,2,1:T(4,128)S(1)}, f32[256,8,4]{0,2,1:T(4,128)S(1)}, f32[256,8,4,128]{3,0,2,1:T(8,128)})) conditional(s32[]{:T(128)} %convert_element_type.61, (f32[256,8,4]{0,2,1:T(4,128)S(1)}, f32[256,8,4]{0,2,1:T(4,128)S(1)}, f32[256,8,4,128]{3,0,2,1:T(8,128)}) %tuple.117, (s32[256]{0:T(256)S(1)}, ...), branch_computations={%region_14.14_spmd, %region_15.17_spmd} | conditional | flops 552616960 | bytes 57675356 | solution.py:73
  152.8 1.1 fusion.32
  154.1 3.7 %bitcast_add_fusion.1 = f32[256,8,4,128]{3,0,2,1:T(8,128)S(1)} fusion(f32[256,8,4,128]{3,0,2,1:T(8,128)S(1)} %copy-done.2, f32[8,128,256,4]{2,1,3,0:T(8,128)S(1)} %get-tuple-element.936, f32[256,8,4]{0,2,1:T(4,128)S(1)} %bitcast.87, f32[256,8,4]{0,2,1:T(4,128)S(1)} %max.14, pred[256]{0:T(512)(128)(4,1)S(1)} %and_not_fusion, ...), kind=kOutput, calls=%fused_computation.32 | convolution fusion | flops 275775488 | bytes 12912128 | tf_op jit(solution)/shard_map/while/body/eval_jaxpr/cond/branch_1_fun/qkgt,tkd->qkgd/dot_general | solution.py:65
  157.8 1.9 %copy-done.3 = f32[256,8,4,128]{3,0,2,1:T(8,128)} copy-done((f32[256,8,4,128]{3,0,2,1:T(8,128)}, f32[256,8,4,128]{3,0,2,1:T(8,128)S(1)}, u32[]{:S(2)}) %copy-start.3) | copy-done | bytes 4194328 | tf_op jit(solution)/shard_map/while/body/eval_jaxpr/cond
  163.1 7.9 %conditional.7 = ((f32[256,8,4]{0,2,1:T(4,128)S(1)}, f32[256,8,4]{0,2,1:T(4,128)S(1)}, f32[256,8,4,128]{3,0,2,1:T(8,128)})) conditional(s32[]{:T(128)} %convert_element_type.61, (f32[256,8,4]{0,2,1:T(4,128)S(1)}, f32[256,8,4]{0,2,1:T(4,128)S(1)}, f32[256,8,4,128]{3,0,2,1:T(8,128)}) %tuple.117, (s32[256]{0:T(256)S(1)}, ...), branch_computations={%region_14.14_spmd, %region_15.17_spmd} | conditional | flops 552616960 | bytes 57675356 | solution.py:73
  164.0 1.1 fusion.32
  165.4 3.7 %bitcast_add_fusion.1 = f32[256,8,4,128]{3,0,2,1:T(8,128)S(1)} fusion(f32[256,8,4,128]{3,0,2,1:T(8,128)S(1)} %copy-done.2, f32[8,128,256,4]{2,1,3,0:T(8,128)S(1)} %get-tuple-element.936, f32[256,8,4]{0,2,1:T(4,128)S(1)} %bitcast.87, f32[256,8,4]{0,2,1:T(4,128)S(1)} %max.14, pred[256]{0:T(512)(128)(4,1)S(1)} %and_not_fusion, ...), kind=kOutput, calls=%fused_computation.32 | convolution fusion | flops 275775488 | bytes 12912128 | tf_op jit(solution)/shard_map/while/body/eval_jaxpr/cond/branch_1_fun/qkgt,tkd->qkgd/dot_general | solution.py:65
  169.1 1.9 %copy-done.3 = f32[256,8,4,128]{3,0,2,1:T(8,128)} copy-done((f32[256,8,4,128]{3,0,2,1:T(8,128)}, f32[256,8,4,128]{3,0,2,1:T(8,128)S(1)}, u32[]{:S(2)}) %copy-start.3) | copy-done | bytes 4194328 | tf_op jit(solution)/shard_map/while/body/eval_jaxpr/cond
  171.0 2.9 %divide_convert_fusion = bf16[256,8,4,128]{3,0,2,1:T(8,128)(2,1)S(1)} fusion(f32[256,8,4,128]{3,0,2,1:T(8,128)} %get-tuple-element.775, f32[256,8,4]{0,2,1:T(4,128)S(1)} %get-tuple-element.776), kind=kLoop, calls=%fused_computation.82 | loop fusion | flops 2097152 | bytes 6324224 | tf_op jit(solution)/shard_map/convert_element_type | solution.py:120
  173.9 2.9 %copy.36 = bf16[256,8,4,128]{3,2,1,0:T(4,128)(2,1)} copy(bf16[256,8,4,128]{3,0,2,1:T(8,128)(2,1)S(1)} %divide_convert_fusion) | data formatting | bytes 4194304 | tf_op jit(solution)/shard_map/convert_element_type | solution.py:120
  (100 shorter events, 18.0 us)
Async XLA Ops:
  6.5 14.8 %copy-start.4 = (bf16[256,8,128]{2,1,0:T(8,128)(2,1)S(1)}, bf16[256,8,128]{2,1,0:T(8,128)(2,1)}, u32[]{:S(2)}) copy-start(bf16[256,8,128]{2,1,0:T(8,128)(2,1)} %param.14) | copy-start | bytes 1572868
  6.5 115.6 %all-reduce.3.cloned.1.call-start = ((), (), s32[]{:S(2)}) async-start(), calls=%async_computation | async-start | bytes 4194304 | tf_op jit(solution)/shard_map/pmax | solution.py:110
  8.5 18.0 %collective-permute-start = (bf16[256,8,128]{2,0,1:T(8,128)(2,1)}, bf16[256,8,128]{2,0,1:T(8,128)(2,1)}, u32[]{:S(2)}, u32[]{:S(2)}) collective-permute-start(bf16[256,8,128]{2,0,1:T(8,128)(2,1)} %copy.29), channel_id=1, source_target_pairs={{0,1},{1,2},{2,3},{3,4},{4,5},{5,6},{6,7},{7,8},{8,9},{9,10},{10,1... | collective-permute-start | bytes 1572872 | tf_op jit(solution)/shard_map/ppermute | solution.py:18
  13.6 15.1 %collective-permute-start.1 = (bf16[256,8,128]{2,0,1:T(8,128)(2,1)}, bf16[256,8,128]{2,0,1:T(8,128)(2,1)}, u32[]{:S(2)}, u32[]{:S(2)}) collective-permute-start(bf16[256,8,128]{2,0,1:T(8,128)(2,1)} %copy.32), channel_id=1, source_target_pairs={{0,1},{1,2},{2,3},{3,4},{4,5},{5,6},{6,7},{7,8},{8,9},{9,10},{10,1... | collective-permute-start | bytes 1572872 | tf_op jit(solution)/shard_map/ppermute | solution.py:18
  21.3 2.4 %copy-start.5 = (s32[16]{0:T(128)S(1)}, s32[16]{0:T(128)}, u32[]{:S(2)}) copy-start(s32[16]{0:T(128)} %param.17) | copy-start | bytes 196
  37.6 3.1 %copy-start = (f32[256,8,4,128]{3,0,2,1:T(8,128)S(1)}, f32[256,8,4,128]{3,0,2,1:T(8,128)}, u32[]{:S(2)}) copy-start(f32[256,8,4,128]{3,0,2,1:T(8,128)} %get-tuple-element.727) | copy-start | bytes 12582916 | tf_op jit(solution)/shard_map/while/body/eval_jaxpr/cond
  44.6 1.9 %copy-start.1 = (f32[256,8,4,128]{3,0,2,1:T(8,128)}, f32[256,8,4,128]{3,0,2,1:T(8,128)S(1)}, u32[]{:S(2)}) copy-start(f32[256,8,4,128]{3,0,2,1:T(8,128)S(1)} %bitcast_add_fusion) | copy-start | bytes 12582916 | tf_op jit(solution)/shard_map/while/body/eval_jaxpr/cond
  48.3 3.1 %copy-start = (f32[256,8,4,128]{3,0,2,1:T(8,128)S(1)}, f32[256,8,4,128]{3,0,2,1:T(8,128)}, u32[]{:S(2)}) copy-start(f32[256,8,4,128]{3,0,2,1:T(8,128)} %get-tuple-element.727) | copy-start | bytes 12582916 | tf_op jit(solution)/shard_map/while/body/eval_jaxpr/cond
  55.4 1.9 %copy-start.1 = (f32[256,8,4,128]{3,0,2,1:T(8,128)}, f32[256,8,4,128]{3,0,2,1:T(8,128)S(1)}, u32[]{:S(2)}) copy-start(f32[256,8,4,128]{3,0,2,1:T(8,128)S(1)} %bitcast_add_fusion) | copy-start | bytes 12582916 | tf_op jit(solution)/shard_map/while/body/eval_jaxpr/cond
  57.3 68.8 %copy-start.6 = (s32[4]{0:T(128)S(1)}, s32[4]{0:T(128)}, u32[]{:S(2)}) copy-start(s32[4]{0:T(128)} %param.16) | copy-start | bytes 52
  129.5 2.2 %copy-start.2 = (f32[256,8,4,128]{3,0,2,1:T(8,128)S(1)}, f32[256,8,4,128]{3,0,2,1:T(8,128)}, u32[]{:S(2)}) copy-start(f32[256,8,4,128]{3,0,2,1:T(8,128)} %get-tuple-element.752) | copy-start | bytes 12582916 | tf_op jit(solution)/shard_map/while/body/eval_jaxpr/cond
  135.4 1.9 %copy-start.3 = (f32[256,8,4,128]{3,0,2,1:T(8,128)}, f32[256,8,4,128]{3,0,2,1:T(8,128)S(1)}, u32[]{:S(2)}) copy-start(f32[256,8,4,128]{3,0,2,1:T(8,128)S(1)} %bitcast_add_fusion.1) | copy-start | bytes 12582916 | tf_op jit(solution)/shard_map/while/body/eval_jaxpr/cond
  140.7 2.2 %copy-start.2 = (f32[256,8,4,128]{3,0,2,1:T(8,128)S(1)}, f32[256,8,4,128]{3,0,2,1:T(8,128)}, u32[]{:S(2)}) copy-start(f32[256,8,4,128]{3,0,2,1:T(8,128)} %get-tuple-element.752) | copy-start | bytes 12582916 | tf_op jit(solution)/shard_map/while/body/eval_jaxpr/cond
  146.6 1.9 %copy-start.3 = (f32[256,8,4,128]{3,0,2,1:T(8,128)}, f32[256,8,4,128]{3,0,2,1:T(8,128)S(1)}, u32[]{:S(2)}) copy-start(f32[256,8,4,128]{3,0,2,1:T(8,128)S(1)} %bitcast_add_fusion.1) | copy-start | bytes 12582916 | tf_op jit(solution)/shard_map/while/body/eval_jaxpr/cond
  151.9 2.2 %copy-start.2 = (f32[256,8,4,128]{3,0,2,1:T(8,128)S(1)}, f32[256,8,4,128]{3,0,2,1:T(8,128)}, u32[]{:S(2)}) copy-start(f32[256,8,4,128]{3,0,2,1:T(8,128)} %get-tuple-element.752) | copy-start | bytes 12582916 | tf_op jit(solution)/shard_map/while/body/eval_jaxpr/cond
  157.8 1.9 %copy-start.3 = (f32[256,8,4,128]{3,0,2,1:T(8,128)}, f32[256,8,4,128]{3,0,2,1:T(8,128)S(1)}, u32[]{:S(2)}) copy-start(f32[256,8,4,128]{3,0,2,1:T(8,128)S(1)} %bitcast_add_fusion.1) | copy-start | bytes 12582916 | tf_op jit(solution)/shard_map/while/body/eval_jaxpr/cond
  163.2 2.2 %copy-start.2 = (f32[256,8,4,128]{3,0,2,1:T(8,128)S(1)}, f32[256,8,4,128]{3,0,2,1:T(8,128)}, u32[]{:S(2)}) copy-start(f32[256,8,4,128]{3,0,2,1:T(8,128)} %get-tuple-element.752) | copy-start | bytes 12582916 | tf_op jit(solution)/shard_map/while/body/eval_jaxpr/cond
  169.1 1.9 %copy-start.3 = (f32[256,8,4,128]{3,0,2,1:T(8,128)}, f32[256,8,4,128]{3,0,2,1:T(8,128)S(1)}, u32[]{:S(2)}) copy-start(f32[256,8,4,128]{3,0,2,1:T(8,128)S(1)} %bitcast_add_fusion.1) | copy-start | bytes 12582916 | tf_op jit(solution)/shard_map/while/body/eval_jaxpr/cond
Sparse Core Ops, SparseCore 0:
  23.8 98.2 all-reduce.2
where the time goes:
time: 185 us; the launch traced here: 184 us
  waiting for transfers between devices  64.8 us (35%)
  local copies, waits for them, and re-layouts  33.3 us (18%)
  matrix products  29.8 us (16%)
  other arithmetic  29.1 us (16%)
  between operations  13.5 us (7%)
  starting transfers between devices  7.73 us (4%)
  loops' own time  5.46 us (3%)
    pmax x1, waiting for transfers between devices, per_device(): key_cube, val_cube = lax.pmax((key_cube, val_cube), 'seq')  64.8 us
    dot_general x6, matrix products, compute(): jnp.einsum('qkgt,tkd->qkgd', exp_terms.astype(jnp.bfloat16), value_block,...  22.7 us
    cond x30, local copies, waits for them, and re-layouts  12.4 us
    unnamed x11, local copies, waits for them, and re-layouts  10.2 us
    ppermute x2, starting transfers between devices, shifted(): return lax.ppermute(shard, axis, pairs)  7.73 us
    dot_general x6, matrix products, compute(): jnp.einsum('qkgd,tkd->qkgt', grouped, key_block, preferred_element_type=j...  7.07 us
    reduce_sum x6, other arithmetic, compute(): denom_sum = denom_sum * factor + jnp.sum(exp_terms, axis=-1)  6.6 us
    reduce_or x8, other arithmetic, update(): return lax.cond(jnp.any(allowed), compute, lambda carried: carried, running)  6.35 us
  transfers between devices with their start and end apart: 3, of which 1 were waited for; matrix products, arithmetic and copies ran while one was open for 19% of the time, Pallas kernels for 0%

commit v1 on v0

v1 whole, which is shorter than its diff:
```python
import functools
import math

import jax
import jax.numpy as jnp
from jax import lax
from jax.experimental import pallas as pl
from jax.experimental.pallas import tpu as pltpu
from jax.sharding import PartitionSpec as P

BLK = 128
WIN = 3

masked_score = -1e30


def shifted(shard, axis, by):
    length = lax.axis_size(axis)
    pairs = [(i, i + by) for i in range(length) if 0 <= i + by < length]
    return lax.ppermute(shard, axis, pairs)


def fill_bias(rank, lens_ref, bias_ref):
    blocks_here, _, span = bias_ref.shape
    for b in range(blocks_here):
        first = (rank * blocks_here + b) * BLK
        query_pos = first + lax.broadcasted_iota(jnp.int32, (BLK, span), 0)
        key_pos = first - (WIN - 1) * BLK + lax.broadcasted_iota(jnp.int32, (BLK, span), 1)

        def step(d, carry):
            end, lowest = carry
            end = end + lens_ref[d]
            return end, jnp.where(query_pos >= end, end, lowest)

        _, lowest = lax.fori_loop(
            0, lens_ref.shape[0], step, (jnp.int32(0), jnp.zeros((BLK, span), jnp.int32))
        )
        seen = (key_pos >= lowest) & (key_pos <= query_pos)
        bias_ref[b] = jnp.where(seen, 0.0, masked_score)


def attn_kernel(ids_ref, lens_ref, q_ref, own_ref, prev_ref, glob_ref, o_ref, bias_ref):
    group_size, tok_rows, head_size = q_ref.shape
    blocks_here = tok_rows // BLK
    rank = lax.axis_index("seq")
    factor = math.log2(math.e) / math.sqrt(head_size)
    rows = group_size * BLK

    @pl.when(pl.program_id(0) == 0)
    def _():
        fill_bias(rank, lens_ref, bias_ref)

    def near(which, b):
        parts = []
        for i in range(blocks_here + b - WIN + 1, blocks_here + b + 1):
            src, j = (prev_ref, i) if i < blocks_here else (own_ref, i - blocks_here)
            parts.append(src[which, 0, j * BLK : (j + 1) * BLK, :])
        return jnp.concatenate(parts, axis=0)

    dims = (((1,), (1,)), ((), ()))
    for b in range(blocks_here):
        q = q_ref[:, b * BLK : (b + 1) * BLK, :].reshape(rows, head_size)
        s_near = lax.dot_general(q, near(0, b), dims, preferred_element_type=jnp.float32)
        s_near = (s_near.reshape(group_size, BLK, WIN * BLK) + bias_ref[b][None]).reshape(
            rows, WIN * BLK
        )
        s_far = lax.dot_general(q, glob_ref[0, 0], dims, preferred_element_type=jnp.float32)
        far = []
        for s in range(ids_ref.shape[0]):
            gap = rank * blocks_here + b - ids_ref[s]
            shift = jnp.where((gap >= 0) & (gap < WIN), masked_score, 0.0)
            far.append(s_far[:, s * BLK : (s + 1) * BLK] + shift)
        scores = jnp.concatenate([s_near] + far, axis=1)
        peak = jnp.max(scores, axis=1, keepdims=True)
        terms = jnp.exp2((scores - peak) * factor)
        total = jnp.sum(terms, axis=1, keepdims=True)
        weights = terms.astype(jnp.bfloat16)
        held = jnp.concatenate([near(1, b), glob_ref[1, 0]], axis=0)
        out = jnp.dot(weights, held, preferred_element_type=jnp.float32) / total
        o_ref[:, b * BLK : (b + 1) * BLK, :] = out.astype(o_ref.dtype).reshape(
            group_size, BLK, head_size
        )


def attention(ids, lens, q, own, prev, glob):
    heads_here, tok_rows, head_size = q.shape
    kv_count = own.shape[1]
    group_size = heads_here // kv_count
    blocks_here = tok_rows // BLK
    smem = pl.BlockSpec(memory_space=pltpu.SMEM)
    q_spec = pl.BlockSpec((group_size, tok_rows, head_size), lambda k: (k, 0, 0))
    keyed = lambda n: pl.BlockSpec((2, 1, n, head_size), lambda k: (0, k, 0, 0))
    return pl.pallas_call(
        attn_kernel,
        grid=(kv_count,),
        out_shape=jax.ShapeDtypeStruct(q.shape, jnp.bfloat16),
        in_specs=[smem, smem, q_spec, keyed(tok_rows), keyed(tok_rows), keyed(glob.shape[2])],
        out_specs=q_spec,
        scratch_shapes=[pltpu.VMEM((blocks_here, BLK, WIN * BLK), jnp.float32)],
    )(ids, lens, q, own, prev, glob)


def per_device(queries, keys, values, global_ids, doc_lengths):
    tok_rows, heads_here, head_size = queries.shape
    kv_count = keys.shape[1]
    blocks_here = tok_rows // BLK
    rank = lax.axis_index("seq")
    own = jnp.stack([keys, values]).transpose(0, 2, 1, 3)
    prev = shifted(own, "seq", 1)
    mine = global_ids // blocks_here == rank
    slots = global_ids % blocks_here
    glob = own.reshape(2, kv_count, blocks_here, BLK, head_size)[:, :, slots]
    lowest = jnp.array(-jnp.inf, jnp.bfloat16)
    glob = jnp.where(mine[None, None, :, None, None], glob, lowest)
    glob = lax.pmax(glob, "seq")
    glob = glob.reshape(2, kv_count, -1, head_size)
    q = queries.transpose(1, 0, 2)
    out = attention(global_ids, doc_lengths, q, own, prev, glob)
    return out.transpose(1, 0, 2)


def solution(mesh):
    tokens = P(("grp", "seq"), None, None)
    return jax.shard_map(
        per_device,
        mesh=mesh,
        in_specs=(tokens, tokens, tokens, P("grp"), P("grp")),
        out_specs=tokens,
        check_vma=False,
    )
```

time: 185 us -> 145 us (0.78)
  waiting for transfers between devices: 64.8 us -> 95.8 us
  matrix products: 29.8 us -> 0 us
  other arithmetic: 29.1 us -> 2.71 us
  local copies, waits for them, and re-layouts: 33.3 us -> 11.4 us
  Pallas kernels: 0 us -> 17.6 us
  loops' own time: 5.46 us -> 0 us
  starting transfers between devices: 7.73 us -> 3.4 us
    pmax x1, waiting for transfers between devices: 64.8 us -> 95.8 us  [per_device(): glob = lax.pmax(glob, 'seq')]
    dot_general x12 -> x0, matrix products: 29.8 us -> none  [the longest x6 22.7 us: compute(): jnp.einsum('qkgt,tkd->qkgd', exp_terms.astype(jnp.bfloat16), value_block,...]
    pallas_call x0 -> x1, Pallas kernels: none -> 17.6 us  [attention(): pl.pallas_call(attn_kernel, grid=(kv_count,), out_shape=jax.ShapeDtypeStr...]
    cond x30 -> x0, local copies, waits for them, and re-layouts: 12.4 us -> none
    reduce_sum x11 -> x0, other arithmetic: 7.04 us -> none  [the longest x6 6.6 us: compute(): denom_sum = denom_sum * factor + jnp.sum(exp_terms, axis=-1)]
    unnamed x11 -> x5, local copies, waits for them, and re-layouts: 10.2 us -> 3.34 us
    reduce_or x8 -> x0, other arithmetic: 6.35 us -> none  [update(): return lax.cond(jnp.any(allowed), compute, lambda carried: carried, running)]
    another operation x10 -> x0, loops' own time: 5.46 us -> none  [the longest x1 2.62 us: per_device(): running = lax.fori_loop(0, 2 * blocks_here, window_turn, running)]
  transfers between devices with their start and end apart: 3 -> 2, of which waited for: 1 -> 1; matrix products, arithmetic and copies ran while one was open for 19% -> 1% of each run, Pallas kernels for 0% -> 0%
where the time goes in v1:
time: 145 us; the launch traced here: 144 us
  waiting for transfers between devices  95.8 us (66%)
  Pallas kernels  17.6 us (12%)
  between operations  13.4 us (9%)
  local copies, waits for them, and re-layouts  11.4 us (8%)
  starting transfers between devices  3.4 us (2%)
  other arithmetic  2.71 us (2%)
    pmax x1, waiting for transfers between devices, per_device(): glob = lax.pmax(glob, 'seq')  95.8 us
    pallas_call x1, Pallas kernels, attention(): pl.pallas_call(attn_kernel, grid=(kv_count,), out_shape=jax.ShapeDtypeStr...  17.6 us
    transpose x1, local copies, waits for them, and re-layouts, per_device(): return out.transpose(1, 0, 2)  4.26 us
    ppermute x1, starting transfers between devices, shifted(): return lax.ppermute(shard, axis, pairs)  3.4 us
    unnamed x5, local copies, waits for them, and re-layouts  3.34 us
  transfers between devices with their start and end apart: 2, of which 1 were waited for; matrix products, arithmetic and copies ran while one was open for 1% of the time, Pallas kernels for 0%

profile of v1, /device:TPU:0, one launch (start us, length us, event | category | flops | bytes accessed | tf_op | source)
XLA Modules:
  0.0 144.3 jit_solution(1057401952422200009)
XLA Ops:
  6.5 0.0 all-reduce.2.cloned.1.call-start
  6.5 0.7 compare_select_fusion
  7.2 0.7 fusion
  7.9 1.4 copy_bitcast_fusion.1
  9.3 1.1 pad_maximum_fusion
  10.4 0.9 gather_fusion
  11.3 0.3 select_bitcast_fusion
  11.6 0.0 copy-start.1
  11.6 1.4 copy.13
  13.1 0.0 copy-start
  13.1 0.0 all-reduce.2.cloned.1.call-update
  13.1 1.2 copy-done
  14.3 3.4 %collective-permute-start = (bf16[2,8,256,128]{3,2,1,0:T(8,128)(2,1)S(1)}, bf16[2,8,256,128]{3,2,1,0:T(8,128)(2,1)}, u32[]{:S(2)}, u32[]{:S(2)}) collective-permute-start(bf16[2,8,256,128]{3,2,1,0:T(8,128)(2,1)S(1)} %copy-done), channel_id=1, source_target_pairs={{0,1},{1,2},{2,3},{3,4},{4,5},{5,6},{6,7},{7,8},{8,9},{9,10},{10,1... | collective-permute-start | bytes 3145736 | tf_op jit(solution)/shard_map/ppermute | solution.py:20
  17.7 0.0 copy-done.1
  17.7 2.1 %copy.18 = bf16[256,32,128]{2,0,1:T(8,128)(2,1)} copy(bf16[256,32,128]{2,1,0:T(8,128)(2,1)S(1)} %copy-done.1) | data formatting | bytes 4194304 | tf_op args[0]
  19.8 95.8 %all-reduce.2.cloned.1.call-done.glob_ref = bf16[2,8,512,128]{3,2,1,0:T(8,128)(2,1)} async-done(((bf16[2,8,512,128]{3,2,1,0:T(8,128)(2,1)}), bf16[2,8,512,128]{3,2,1,0:T(8,128)(2,1)}) %all-reduce.2.cloned.1.call-update) | async-done | bytes 2097168 | tf_op jit(solution)/shard_map/pmax | solution.py:115
  115.6 0.0 collective-permute-done.prev_ref
  115.6 17.6 %shard_map.55 = bf16[32,256,128]{2,1,0:T(8,128)(2,1)} custom-call(s32[4]{0:T(128)} %ids_ref.1, s32[16]{0:T(128)} %lens_ref.1, bf16[32,256,128]{2,1,0:T(8,128)(2,1)} %bitcast.16, bf16[2,8,256,128]{3,2,1,0:T(8,128)(2,1)} %get-tuple-element.6.own_ref, bf16[2,8,256,128]{3,2,1,0:T(8,128)(2,1)} %collective-permute-done.prev_ref, ...), custom_call_target="tpu_custom_call" | custom-call | tf_op jit(solution)/shard_map/pallas_call | solution.py:93
  133.2 4.3 %copy.14 = bf16[256,32,128]{2,1,0:T(8,128)(2,1)} copy(bf16[256,32,128]{2,0,1:T(8,128)(2,1)} %bitcast.17) | data formatting | bytes 4194304 | tf_op jit(solution)/shard_map/transpose | solution.py:119
  (1 shorter events, 0.0 us)
Async XLA Ops:
  6.5 109.1 %all-reduce.2.cloned.1.call-start = ((), (), s32[]{:S(2)}) async-start(), calls=%async_computation | async-start | bytes 4194304 | tf_op jit(solution)/shard_map/pmax | solution.py:115
  11.6 6.1 %copy-start.1 = (bf16[256,32,128]{2,1,0:T(8,128)(2,1)S(1)}, bf16[256,32,128]{2,1,0:T(8,128)(2,1)}, u32[]{:S(2)}) copy-start(bf16[256,32,128]{2,1,0:T(8,128)(2,1)} %param.5) | copy-start | bytes 6291460
  13.1 1.2 copy-start
  14.3 101.3 %collective-permute-start = (bf16[2,8,256,128]{3,2,1,0:T(8,128)(2,1)S(1)}, bf16[2,8,256,128]{3,2,1,0:T(8,128)(2,1)}, u32[]{:S(2)}, u32[]{:S(2)}) collective-permute-start(bf16[2,8,256,128]{3,2,1,0:T(8,128)(2,1)S(1)} %copy-done), channel_id=1, source_target_pairs={{0,1},{1,2},{2,3},{3,4},{4,5},{5,6},{6,7},{7,8},{8,9},{9,10},{10,1... | collective-permute-start | bytes 3145736 | tf_op jit(solution)/shard_map/ppermute | solution.py:20
Sparse Core Ops, SparseCore 0:
  13.2 102.3 all-reduce.1

commit v2 on v1

--- a/solution.py
+++ b/solution.py
@@ -12,12 +12,6 @@
 WIN = 3
 
 masked_score = -1e30
-
-
-def shifted(shard, axis, by):
-    length = lax.axis_size(axis)
-    pairs = [(i, i + by) for i in range(length) if 0 <= i + by < length]
-    return lax.ppermute(shard, axis, pairs)
 
 
 def fill_bias(rank, lens_ref, bias_ref):
@@ -100,20 +94,156 @@
     )(ids, lens, q, own, prev, glob)
 
 
+def exchange_kernel(n, ids_ref, own_ref, prev_ref, glob_ref, raw_ref, to_sem, from_sem, pass_sem, land_sem, near_sem):
+    rank = lax.axis_index("seq")
+    blocks_here, parts = own_ref.shape[1], own_ref.shape[2]
+    lines = n // 4
+    line, low = rank // 4, rank % 4
+    pair = line * 4 + (low + 2) % 4
+    partner = rank + 1 - 2 * (rank % 2)
+
+    barrier = pltpu.get_barrier_semaphore()
+
+    def greet(i, carry):
+        pl.semaphore_signal(
+            barrier, inc=1, device_id={"seq": (rank + i) % n}, device_id_type=pl.DeviceIdType.MESH
+        )
+        return carry
+
+    lax.fori_loop(1, n, greet, 0)
+    pl.semaphore_wait(barrier, n - 1)
+
+    def remote(src, dst, send, recv, device):
+        return pltpu.make_async_remote_copy(
+            src_ref=src,
+            dst_ref=dst,
+            send_sem=send,
+            recv_sem=recv,
+            device_id={"seq": device},
+            device_id_type=pl.DeviceIdType.MESH,
+        )
+
+    def gather(i):
+        dest = (rank + i) % n
+        return remote(
+            own_ref.at[dest // parts, :, dest % parts],
+            raw_ref.at[pl.ds(rank * blocks_here, blocks_here)],
+            to_sem.at[i],
+            from_sem.at[i],
+            dest,
+        )
+
+    def spread(i, piece, device):
+        region = glob_ref.at[piece // parts, :, piece % parts]
+        return remote(region, region, pass_sem.at[i], land_sem.at[i], device)
+
+    def loop(low_end, high_end, body):
+        def step(i, carry):
+            body(i)
+            return carry
+
+        lax.fori_loop(low_end, high_end, step, 0)
+
+    near = remote(own_ref, prev_ref, near_sem.at[0], near_sem.at[1], (rank + 1) % n)
+    loop(1, n, lambda i: gather(i).start())
+
+    @pl.when(rank < n - 1)
+    def _():
+        near.start()
+
+    @pl.when(rank == 0)
+    def _():
+        prev_ref[...] = jnp.zeros_like(prev_ref)
+
+    raw_ref[pl.ds(rank * blocks_here, blocks_here)] = own_ref[rank // parts, :, rank % parts]
+    loop(1, n, lambda i: gather(i).wait_recv())
+    for s in range(ids_ref.shape[0]):
+        glob_ref[rank // parts, s, rank % parts] = raw_ref[ids_ref[s]]
+
+    mine = lambda j: ((line - j + lines) % lines) * 4 + low
+    theirs = lambda j: ((line - j + lines) % lines) * 4 + (low + 2) % 4
+    ahead = lambda j: ((line + j) % lines) * 4 + low
+    along = lambda j: spread(j, rank, ahead(j))
+    across = lambda j: spread(lines + j, mine(j), pair)
+    over = lambda j: spread(2 * lines + j, mine(j), partner)
+    last = lambda j: spread(3 * lines + j, theirs(j), partner)
+
+    loop(1, lines, lambda j: along(j).start())
+
+    def first_turn(j):
+        @pl.when(j > 0)
+        def _():
+            along(j).wait_recv()
+
+        across(j).start()
+        over(j).start()
+
+    loop(0, lines, first_turn)
+
+    def second_turn(j):
+        across(j).wait_recv()
+        last(j).start()
+
+    loop(0, lines, second_turn)
+
+    def final_turn(j):
+        over(j).wait_recv()
+        last(j).wait_recv()
+        across(j).wait_send()
+        over(j).wait_send()
+        last(j).wait_send()
+
+    loop(0, lines, final_turn)
+    loop(1, lines, lambda j: along(j).wait_send())
+    loop(1, n, lambda i: gather(i).wait_send())
+
+    @pl.when(rank < n - 1)
+    def _():
+        near.wait_send()
+
+    @pl.when(rank > 0)
+    def _():
+        near.wait_recv()
+
+
+def exchange(ids, own):
+    n = lax.axis_size("seq")
+    _, kv_count, tok_rows, head_size = own.shape
+    sides = 2 * kv_count
+    parts = n // sides
+    part_rows = BLK // parts
+    blocks_here = tok_rows // BLK
+    own = own.reshape(sides, blocks_here, parts, part_rows, head_size)
+    slots = ids.shape[0]
+    vmem = pl.BlockSpec(memory_space=pltpu.VMEM)
+    dma = pltpu.SemaphoreType.DMA
+    prev, glob = pl.pallas_call(
+        functools.partial(exchange_kernel, n),
+        out_shape=(
+            jax.ShapeDtypeStruct(own.shape, own.dtype),
+            jax.ShapeDtypeStruct((sides, slots, parts, part_rows, head_size), own.dtype),
+        ),
+        in_specs=[pl.BlockSpec(memory_space=pltpu.SMEM), vmem],
+        out_specs=(vmem, vmem),
+        scratch_shapes=[
+            pltpu.VMEM((n * blocks_here, part_rows, head_size), own.dtype),
+            dma((n,)),
+            dma((n,)),
+            dma((n,)),
+            dma((n,)),
+            dma((2,)),
+        ],
+        compiler_params=pltpu.CompilerParams(collective_id=0, has_side_effects=True),
+    )(ids, own)
+    return (
+        prev.reshape(2, kv_count, tok_rows, head_size),
+        glob.reshape(2, kv_count, slots * BLK, head_size),
+    )
+
+
 def per_device(queries, keys, values, global_ids, doc_lengths):
-    tok_rows, heads_here, head_size = queries.shape
-    kv_count = keys.shape[1]
-    blocks_here = tok_rows // BLK
-    rank = lax.axis_index("seq")
     own = jnp.stack([keys, values]).transpose(0, 2, 1, 3)
-    prev = shifted(own, "seq", 1)
-    mine = global_ids // blocks_here == rank
-    slots = global_ids % blocks_here
-    glob = own.reshape(2, kv_count, blocks_here, BLK, head_size)[:, :, slots]
-    lowest = jnp.array(-jnp.inf, jnp.bfloat16)
-    glob = jnp.where(mine[None, None, :, None, None], glob, lowest)
-    glob = lax.pmax(glob, "seq")
-    glob = glob.reshape(2, kv_count, -1, head_size)
+    prev, glob = exchange(global_ids, own)
     q = queries.transpose(1, 0, 2)
     out = attention(global_ids, doc_lengths, q, own, prev, glob)
     return out.transpose(1, 0, 2)

time: 145 us -> 86.7 us (0.60)
  waiting for transfers between devices: 95.8 us -> 0 us
  Pallas kernels: 17.6 us -> 74.9 us
  between operations: 13.4 us -> 0.03 us
  starting transfers between devices: 3.4 us -> 0 us
  local copies, waits for them, and re-layouts: 11.4 us -> 8.65 us
    pmax x1 -> x0, waiting for transfers between devices: 95.8 us -> none  [per_device(): glob = lax.pmax(glob, 'seq')]
    pallas_call x0 -> x1, Pallas kernels: none -> 57.4 us  [exchange(): pl.pallas_call(functools.partial(exchange_kernel, n), out_shape=(jax.Shap...]
    ppermute x1 -> x0, starting transfers between devices: 3.4 us -> none  [shifted(): return lax.ppermute(shard, axis, pairs)]
    unnamed x5 -> x3, local copies, waits for them, and re-layouts: 3.34 us -> 3 us
  transfers between devices with their start and end apart: 2 -> 0, of which waited for: 1 -> 0; matrix products, arithmetic and copies ran while one was open for 1% -> 0% of each run, Pallas kernels for 0% -> 0%
where the time goes in v2:
time: 86.7 us; the launch traced here: 85.1 us
  Pallas kernels  74.9 us (86%)
  local copies, waits for them, and re-layouts  8.65 us (10%)
  other arithmetic  1.47 us (2%)
    pallas_call x1, Pallas kernels, exchange(): pl.pallas_call(functools.partial(exchange_kernel, n), out_shape=(jax.Shap...  57.4 us
    pallas_call x1, Pallas kernels, attention(): pl.pallas_call(attn_kernel, grid=(kv_count,), out_shape=jax.ShapeDtypeStr...  17.6 us
    transpose x1, local copies, waits for them, and re-layouts, per_device(): return out.transpose(1, 0, 2)  4.26 us
    unnamed x3, local copies, waits for them, and re-layouts  3 us

profile of v2, /device:TPU:0, one launch (start us, length us, event | category | flops | bytes accessed | tf_op | source)
XLA Modules:
  0.0 85.1 jit_solution(1225021866109215558)
XLA Ops:
  0.0 1.4 %copy_bitcast_fusion.1 = (bf16[1,256,8,128]{3,1,2,0:T(8,128)(2,1)S(1)}, bf16[1,256,8,128]{3,1,2,0:T(8,128)(2,1)S(1)}) fusion(bf16[256,8,128]{2,1,0:T(8,128)(2,1)} %param.7, bf16[256,8,128]{2,1,0:T(8,128)(2,1)} %param.6), kind=kLoop, calls=%fused_computation.2 | loop fusion | bytes 2097152 | tf_op jit(solution)/shard_map/stack | solution.py:245
  1.4 0.0 copy-start
  1.4 1.5 %pad_maximum_fusion = (bf16[2,256,8,128]{3,1,2,0:T(8,128)(2,1)}, bf16[2,8,256,128]{3,2,1,0:T(8,128)(2,1)}) fusion(bf16[1,256,8,128]{3,1,2,0:T(8,128)(2,1)S(1)} %get-tuple-element.11, bf16[1,256,8,128]{3,1,2,0:T(8,128)(2,1)S(1)} %get-tuple-element.12), kind=kLoop, calls=%fused_computation.1 | loop fusion | flops 524288 | bytes 3145728 | tf_op jit(solution)/shard_map/stack | solution.py:245
  2.9 0.9 %copy-done = bf16[256,32,128]{2,1,0:T(8,128)(2,1)S(1)} copy-done((bf16[256,32,128]{2,1,0:T(8,128)(2,1)S(1)}, bf16[256,32,128]{2,1,0:T(8,128)(2,1)}, u32[]{:S(2)}) %copy-start) | copy-done | bytes 2097176
  3.7 2.1 %copy.14 = bf16[256,32,128]{2,0,1:T(8,128)(2,1)} copy(bf16[256,32,128]{2,1,0:T(8,128)(2,1)S(1)} %copy-done) | data formatting | bytes 4194304 | tf_op args[0]
  5.9 57.4 %shard_map.55 = (bf16[16,2,1,128,128]{4,3,2,1,0:T(8,128)(2,1)}, bf16[16,4,1,128,128]{4,3,2,1,0:T(8,128)(2,1)}) custom-call(s32[4]{0:T(128)} %ids_ref.3, bf16[16,2,1,128,128]{4,3,2,1,0:T(8,128)(2,1)} %bitcast.18), custom_call_target="tpu_custom_call" | custom-call | tf_op jit(solution)/shard_map/pallas_call | solution.py:220
  63.3 17.6 %shard_map.56 = bf16[32,256,128]{2,1,0:T(8,128)(2,1)} custom-call(s32[4]{0:T(128)} %ids_ref.3, s32[16]{0:T(128)} %lens_ref.1, bf16[32,256,128]{2,1,0:T(8,128)(2,1)} %bitcast.16, bf16[2,8,256,128]{3,2,1,0:T(8,128)(2,1)} %get-tuple-element.10.own_ref, bf16[2,8,256,128]{3,2,1,0:T(8,128)(2,1)} %bitcast.20, bf16[2,8,512,128]{3,2,1,0:T(8,128)(2,1)} %bitcast.19), custom_call_target="tpu_custom_call" | custom-call | tf_op jit(solution)/shard_map/pallas_call | solution.py:87
  80.8 4.3 %copy.10 = bf16[256,32,128]{2,1,0:T(8,128)(2,1)} copy(bf16[256,32,128]{2,0,1:T(8,128)(2,1)} %bitcast.17) | data formatting | bytes 4194304 | tf_op jit(solution)/shard_map/transpose | solution.py:249
Async XLA Ops:
  1.4 2.4 %copy-start = (bf16[256,32,128]{2,1,0:T(8,128)(2,1)S(1)}, bf16[256,32,128]{2,1,0:T(8,128)(2,1)}, u32[]{:S(2)}) copy-start(bf16[256,32,128]{2,1,0:T(8,128)(2,1)} %param.5) | copy-start | bytes 6291460

commit v3 on v2

v3 whole, which is shorter than its diff:
```python
import functools
import math

import jax
import jax.numpy as jnp
from jax import lax
from jax.experimental import pallas as pl
from jax.experimental.pallas import tpu as pltpu
from jax.sharding import PartitionSpec as P

BLK = 128
WIN = 3

masked_score = -1e30


def fill_bias(rank, lens_ref, bias_ref):
    blocks_here, _, span = bias_ref.shape
    for b in range(blocks_here):
        first = (rank * blocks_here + b) * BLK
        query_pos = first + lax.broadcasted_iota(jnp.int32, (BLK, span), 0)
        key_pos = first - (WIN - 1) * BLK + lax.broadcasted_iota(jnp.int32, (BLK, span), 1)

        def step(d, carry):
            end, lowest = carry
            end = end + lens_ref[d]
            return end, jnp.where(query_pos >= end, end, lowest)

        _, lowest = lax.fori_loop(
            0, lens_ref.shape[0], step, (jnp.int32(0), jnp.zeros((BLK, span), jnp.int32))
        )
        seen = (key_pos >= lowest) & (key_pos <= query_pos)
        bias_ref[b] = jnp.where(seen, 0.0, masked_score)


def fused_kernel(
    n,
    ids_ref,
    lens_ref,
    q_ref,
    own_ref,
    o_ref,
    prev_ref,
    glob_ref,
    raw_ref,
    bias_ref,
    peak_ref,
    total_ref,
    sum_ref,
    to_sem,
    from_sem,
    pass_sem,
    land_sem,
    near_sem,
):
    rank = lax.axis_index("seq")
    blocks_here, parts = own_ref.shape[1], own_ref.shape[2]
    lines = n // 4
    line, low = rank // 4, rank % 4
    pair = line * 4 + (low + 2) % 4
    partner = rank + 1 - 2 * (rank % 2)

    barrier = pltpu.get_barrier_semaphore()

    def greet(i, carry):
        pl.semaphore_signal(
            barrier, inc=1, device_id={"seq": (rank + i) % n}, device_id_type=pl.DeviceIdType.MESH
        )
        return carry

    lax.fori_loop(1, n, greet, 0)
    pl.semaphore_wait(barrier, n - 1)

    def remote(src, dst, send, recv, device):
        return pltpu.make_async_remote_copy(
            src_ref=src,
            dst_ref=dst,
            send_sem=send,
            recv_sem=recv,
            device_id={"seq": device},
            device_id_type=pl.DeviceIdType.MESH,
        )

    def gather(i):
        dest = (rank + i) % n
        return remote(
            own_ref.at[dest // parts, :, dest % parts],
            raw_ref.at[pl.ds(rank * blocks_here, blocks_here)],
            to_sem.at[i],
            from_sem.at[i],
            dest,
        )

    def spread(i, piece, device):
        region = glob_ref.at[piece // parts, :, piece % parts]
        return remote(region, region, pass_sem.at[i], land_sem.at[i], device)

    def loop(low_end, high_end, body):
        def step(i, carry):
            body(i)
            return carry

        lax.fori_loop(low_end, high_end, step, 0)

    near = remote(own_ref, prev_ref, near_sem.at[0], near_sem.at[1], (rank + 1) % n)
    loop(1, n, lambda i: gather(i).start())

    kv_count = own_ref.shape[0] // 2
    head_size = own_ref.shape[-1]
    group_size = q_ref.shape[0] // kv_count
    rows = group_size * BLK
    factor = math.log2(math.e) / math.sqrt(head_size)
    dims = (((1,), (1,)), ((), ()))

    def scores_of(k, b, keys):
        q = q_ref[pl.ds(k * group_size, group_size), b * BLK : (b + 1) * BLK, :]
        return lax.dot_general(
            q.reshape(rows, head_size), keys, dims, preferred_element_type=jnp.float32
        )

    def masked(scores, bias):
        wide = scores.reshape(group_size, BLK, scores.shape[1]) + bias[None]
        return wide.reshape(scores.shape)

    def absorb(k, b, scores, held, first=False):
        peak = jnp.max(scores, axis=1, keepdims=True)
        if not first:
            old = peak_ref[k, b]
            peak = jnp.maximum(peak, old)
        terms = jnp.exp2((scores - peak) * factor)
        total = jnp.sum(terms, axis=1, keepdims=True)
        out = jnp.dot(terms.astype(jnp.bfloat16), held, preferred_element_type=jnp.float32)
        if not first:
            fade = jnp.exp2((old - peak) * factor)
            total = total + total_ref[k, b] * fade
            out = out + sum_ref[k, b] * fade
        return peak, total, out

    def keep(k, b, state):
        peak_ref[k, b], total_ref[k, b], sum_ref[k, b] = state

    fill_bias(rank, lens_ref, bias_ref)

    def own_turn(k):
        for b in range(blocks_here):
            first = max(0, b - WIN + 1)
            count = b + 1 - first
            keys = own_ref[k, first : b + 1].reshape(count * BLK, head_size)
            held = own_ref[kv_count + k, first : b + 1].reshape(count * BLK, head_size)
            scores = masked(scores_of(k, b, keys), bias_ref[b][:, (WIN - count) * BLK :])
            keep(k, b, absorb(k, b, scores, held, first=True))

    loop(0, kv_count, own_turn)

    @pl.when(rank == 0)
    def _():
        prev_ref[...] = jnp.zeros_like(prev_ref)

    raw_ref[pl.ds(rank * blocks_here, blocks_here)] = own_ref[rank // parts, :, rank % parts]
    loop(1, n, lambda i: gather(i).wait_recv())
    for s in range(ids_ref.shape[0]):
        glob_ref[rank // parts, s, rank % parts] = raw_ref[ids_ref[s]]

    mine = lambda j: ((line - j + lines) % lines) * 4 + low
    theirs = lambda j: ((line - j + lines) % lines) * 4 + (low + 2) % 4
    ahead = lambda j: ((line + j) % lines) * 4 + low
    along = lambda j: spread(j, rank, ahead(j))
    across = lambda j: spread(lines + j, mine(j), pair)
    over = lambda j: spread(2 * lines + j, mine(j), partner)
    last = lambda j: spread(3 * lines + j, theirs(j), partner)

    loop(1, lines, lambda j: along(j).start())

    def first_turn(j):
        @pl.when(j > 0)
        def _():
            along(j).wait_recv()

        across(j).start()
        over(j).start()

    loop(0, lines, first_turn)

    def second_turn(j):
        across(j).wait_recv()
        last(j).start()

    loop(0, lines, second_turn)

    def final_turn(j):
        over(j).wait_recv()
        last(j).wait_recv()
        across(j).wait_send()
        over(j).wait_send()
        last(j).wait_send()

    @pl.when(rank < n - 1)
    def _():
        near.start()

    loop(0, lines, final_turn)

    def far_turn(k):
        keys = glob_ref[k].reshape(-1, head_size)
        held = glob_ref[kv_count + k].reshape(-1, head_size)
        for b in range(blocks_here):
            scores = scores_of(k, b, keys)
            far = []
            for s in range(ids_ref.shape[0]):
                gap = rank * blocks_here + b - ids_ref[s]
                shift = jnp.where((gap >= 0) & (gap < WIN), masked_score, 0.0)
                far.append(scores[:, s * BLK : (s + 1) * BLK] + shift)
            keep(k, b, absorb(k, b, jnp.concatenate(far, axis=1), held))

    loop(0, kv_count, far_turn)
    loop(1, lines, lambda j: along(j).wait_send())
    loop(1, n, lambda i: gather(i).wait_send())

    @pl.when(rank < n - 1)
    def _():
        near.wait_send()

    @pl.when(rank > 0)
    def _():
        near.wait_recv()

    def near_turn(k):
        for b in range(blocks_here):
            count = max(0, WIN - 1 - b)
            if count:
                keys = prev_ref[k, blocks_here - count :].reshape(count * BLK, head_size)
                held = prev_ref[kv_count + k, blocks_here - count :].reshape(count * BLK, head_size)
                scores = masked(scores_of(k, b, keys), bias_ref[b][:, : count * BLK])
                _, total, out = absorb(k, b, scores, held)
            else:
                total, out = total_ref[k, b], sum_ref[k, b]
            out = (out / total).astype(o_ref.dtype).reshape(group_size, BLK, head_size)
            o_ref[pl.ds(k * group_size, group_size), b * BLK : (b + 1) * BLK, :] = out

    loop(0, kv_count, near_turn)


def fused(ids, lens, q, own):
    n = lax.axis_size("seq")
    _, kv_count, tok_rows, head_size = own.shape
    sides = 2 * kv_count
    parts = n // sides
    part_rows = BLK // parts
    blocks_here = tok_rows // BLK
    rows = q.shape[0] // kv_count * BLK
    own = own.reshape(sides, blocks_here, parts, part_rows, head_size)
    smem = pl.BlockSpec(memory_space=pltpu.SMEM)
    vmem = pl.BlockSpec(memory_space=pltpu.VMEM)
    dma = pltpu.SemaphoreType.DMA
    return pl.pallas_call(
        functools.partial(fused_kernel, n),
        out_shape=jax.ShapeDtypeStruct(q.shape, q.dtype),
        in_specs=[smem, smem, vmem, vmem],
        out_specs=vmem,
        scratch_shapes=[
            pltpu.VMEM(own.shape, own.dtype),
            pltpu.VMEM((sides, ids.shape[0], parts, part_rows, head_size), own.dtype),
            pltpu.VMEM((n * blocks_here, part_rows, head_size), own.dtype),
            pltpu.VMEM((blocks_here, BLK, WIN * BLK), jnp.float32),
            pltpu.VMEM((kv_count, blocks_here, rows, 1), jnp.float32),
            pltpu.VMEM((kv_count, blocks_here, rows, 1), jnp.float32),
            pltpu.VMEM((kv_count, blocks_here, rows, head_size), jnp.float32),
            dma((n,)),
            dma((n,)),
            dma((n,)),
            dma((n,)),
            dma((2,)),
        ],
        compiler_params=pltpu.CompilerParams(collective_id=0, has_side_effects=True),
    )(ids, lens, q, own)


def per_device(queries, keys, values, global_ids, doc_lengths):
    own = jnp.stack([keys, values]).transpose(0, 2, 1, 3)
    q = queries.transpose(1, 0, 2)
    return fused(global_ids, doc_lengths, q, own).transpose(1, 0, 2)


def solution(mesh):
    tokens = P(("grp", "seq"), None, None)
    return jax.shard_map(
        per_device,
        mesh=mesh,
        in_specs=(tokens, tokens, tokens, P("grp"), P("grp")),
        out_specs=tokens,
        check_vma=False,
    )
```

time: 86.7 us -> 113 us (1.30)
  the two profiles are of different devices: /device:TPU:0 before, /device:TPU:11 now
where the time goes in v3:
time: 113 us
  Pallas kernels  104 us (92%)
  local copies, waits for them, and re-layouts  7.59 us (7%)
  other arithmetic  1.45 us (1%)
    pallas_call x1, Pallas kernels, fused(): pl.pallas_call(functools.partial(fused_kernel, n), out_shape=jax.ShapeDty...  104 us
    transpose x1, local copies, waits for them, and re-layouts, per_device(): return fused(global_ids, doc_lengths, q, own).transpose(1, 0, 2)  4.26 us

profile of v3, /device:TPU:11, one launch (start us, length us, event | category | flops | bytes accessed | tf_op | source)
XLA Modules:
  0.0 113.0 jit_solution(9144067984561242908)
XLA Ops:
  0.0 0.0 copy-start
  0.0 1.4 %maximum_bitcast_fusion = bf16[2,8,256,128]{3,1,2,0:T(8,128)(2,1)S(1)} fusion(bf16[1,256,8,128]{3,2,1,0:T(8,128)(2,1)} %bitcast.12, bf16[1,256,8,128]{3,2,1,0:T(8,128)(2,1)} %bitcast.13), kind=kLoop, calls=%fused_computation.1 | loop fusion | flops 524288 | bytes 2097152 | tf_op jit(solution)/shard_map/transpose | solution.py:279
  1.5 1.2 %copy.7 = bf16[2,8,256,128]{3,2,1,0:T(8,128)(2,1)} copy(bf16[2,8,256,128]{3,1,2,0:T(8,128)(2,1)S(1)} %maximum_bitcast_fusion) | data formatting | bytes 2097152 | tf_op jit(solution)/shard_map/transpose | solution.py:279
  2.6 0.0 copy-done
  2.6 2.1 %copy.10 = bf16[256,32,128]{2,0,1:T(8,128)(2,1)} copy(bf16[256,32,128]{2,1,0:T(8,128)(2,1)S(1)} %copy-done) | data formatting | bytes 4194304 | tf_op args[0]
  4.8 104.0 %shard_map.55 = bf16[32,256,128]{2,1,0:T(8,128)(2,1)} custom-call(s32[4]{0:T(128)} %ids_ref.1, s32[16]{0:T(128)} %lens_ref.1, bf16[32,256,128]{2,1,0:T(8,128)(2,1)} %bitcast.10, bf16[16,2,1,128,128]{4,3,2,1,0:T(8,128)(2,1)} %bitcast.11), custom_call_target="tpu_custom_call" | custom-call | tf_op jit(solution)/shard_map/pallas_call | solution.py:255
  108.8 4.3 %copy.8 = bf16[256,32,128]{2,1,0:T(8,128)(2,1)} copy(bf16[256,32,128]{2,0,1:T(8,128)(2,1)} %bitcast.9) | data formatting | bytes 4194304 | tf_op jit(solution)/shard_map/transpose | solution.py:281
Async XLA Ops:
  0.0 2.6 %copy-start = (bf16[256,32,128]{2,1,0:T(8,128)(2,1)S(1)}, bf16[256,32,128]{2,1,0:T(8,128)(2,1)}, u32[]{:S(2)}) copy-start(bf16[256,32,128]{2,1,0:T(8,128)(2,1)} %param.5) | copy-start | bytes 6291460

commit v4 on v2

--- a/solution.py
+++ b/solution.py
@@ -67,10 +67,11 @@
         scores = jnp.concatenate([s_near] + far, axis=1)
         peak = jnp.max(scores, axis=1, keepdims=True)
         terms = jnp.exp2((scores - peak) * factor)
-        total = jnp.sum(terms, axis=1, keepdims=True)
         weights = terms.astype(jnp.bfloat16)
         held = jnp.concatenate([near(1, b), glob_ref[1, 0]], axis=0)
-        out = jnp.dot(weights, held, preferred_element_type=jnp.float32) / total
+        held = jnp.concatenate([held, jnp.ones_like(held)], axis=1)
+        both = jnp.dot(weights, held, preferred_element_type=jnp.float32)
+        out = both[:, :head_size] / both[:, head_size:]
         o_ref[:, b * BLK : (b + 1) * BLK, :] = out.astype(o_ref.dtype).reshape(
             group_size, BLK, head_size
         )

time: 86.7 us -> 84.2 us (0.971)
  Pallas kernels: 74.9 us -> 72.4 us
    pallas_call x1, Pallas kernels: 17.6 us -> 15 us  [attention(): pl.pallas_call(attn_kernel, grid=(kv_count,), out_shape=jax.ShapeDtypeStr...]
where the time goes in v4:
time: 84.2 us; the launch traced here: 82.6 us
  Pallas kernels  72.4 us (86%)
  local copies, waits for them, and re-layouts  8.65 us (10%)
  other arithmetic  1.47 us (2%)
    pallas_call x1, Pallas kernels, exchange(): pl.pallas_call(functools.partial(exchange_kernel, n), out_shape=(jax.Shap...  57.4 us
    pallas_call x1, Pallas kernels, attention(): pl.pallas_call(attn_kernel, grid=(kv_count,), out_shape=jax.ShapeDtypeStr...  15 us
    transpose x1, local copies, waits for them, and re-layouts, per_device(): return out.transpose(1, 0, 2)  4.26 us
    unnamed x3, local copies, waits for them, and re-layouts  3 us

profile of v4, /device:TPU:0, one launch (start us, length us, event | category | flops | bytes accessed | tf_op | source)
XLA Modules:
  0.0 82.6 jit_solution(3622538936582006992)
XLA Ops:
  0.0 1.4 %copy_bitcast_fusion.1 = (bf16[1,256,8,128]{3,1,2,0:T(8,128)(2,1)S(1)}, bf16[1,256,8,128]{3,1,2,0:T(8,128)(2,1)S(1)}) fusion(bf16[256,8,128]{2,1,0:T(8,128)(2,1)} %param.7, bf16[256,8,128]{2,1,0:T(8,128)(2,1)} %param.6), kind=kLoop, calls=%fused_computation.2 | loop fusion | bytes 2097152 | tf_op jit(solution)/shard_map/stack | solution.py:246
  1.4 0.0 copy-start
  1.4 1.5 %pad_maximum_fusion = (bf16[2,256,8,128]{3,1,2,0:T(8,128)(2,1)}, bf16[2,8,256,128]{3,2,1,0:T(8,128)(2,1)}) fusion(bf16[1,256,8,128]{3,1,2,0:T(8,128)(2,1)S(1)} %get-tuple-element.11, bf16[1,256,8,128]{3,1,2,0:T(8,128)(2,1)S(1)} %get-tuple-element.12), kind=kLoop, calls=%fused_computation.1 | loop fusion | flops 524288 | bytes 3145728 | tf_op jit(solution)/shard_map/stack | solution.py:246
  2.9 0.9 %copy-done = bf16[256,32,128]{2,1,0:T(8,128)(2,1)S(1)} copy-done((bf16[256,32,128]{2,1,0:T(8,128)(2,1)S(1)}, bf16[256,32,128]{2,1,0:T(8,128)(2,1)}, u32[]{:S(2)}) %copy-start) | copy-done | bytes 2097176
  3.7 2.1 %copy.14 = bf16[256,32,128]{2,0,1:T(8,128)(2,1)} copy(bf16[256,32,128]{2,1,0:T(8,128)(2,1)S(1)} %copy-done) | data formatting | bytes 4194304 | tf_op args[0]
  5.9 57.4 %shard_map.55 = (bf16[16,2,1,128,128]{4,3,2,1,0:T(8,128)(2,1)}, bf16[16,4,1,128,128]{4,3,2,1,0:T(8,128)(2,1)}) custom-call(s32[4]{0:T(128)} %ids_ref.3, bf16[16,2,1,128,128]{4,3,2,1,0:T(8,128)(2,1)} %bitcast.18), custom_call_target="tpu_custom_call" | custom-call | tf_op jit(solution)/shard_map/pallas_call | solution.py:221
  63.3 15.0 %shard_map.56 = bf16[32,256,128]{2,1,0:T(8,128)(2,1)} custom-call(s32[4]{0:T(128)} %ids_ref.3, s32[16]{0:T(128)} %lens_ref.1, bf16[32,256,128]{2,1,0:T(8,128)(2,1)} %bitcast.16, bf16[2,8,256,128]{3,2,1,0:T(8,128)(2,1)} %get-tuple-element.10.own_ref, bf16[2,8,256,128]{3,2,1,0:T(8,128)(2,1)} %bitcast.20, bf16[2,8,512,128]{3,2,1,0:T(8,128)(2,1)} %bitcast.19), custom_call_target="tpu_custom_call" | custom-call | tf_op jit(solution)/shard_map/pallas_call | solution.py:88
  78.3 4.3 %copy.10 = bf16[256,32,128]{2,1,0:T(8,128)(2,1)} copy(bf16[256,32,128]{2,0,1:T(8,128)(2,1)} %bitcast.17) | data formatting | bytes 4194304 | tf_op jit(solution)/shard_map/transpose | solution.py:250
Async XLA Ops:
  1.4 2.4 %copy-start = (bf16[256,32,128]{2,1,0:T(8,128)(2,1)S(1)}, bf16[256,32,128]{2,1,0:T(8,128)(2,1)}, u32[]{:S(2)}) copy-start(bf16[256,32,128]{2,1,0:T(8,128)(2,1)} %param.5) | copy-start | bytes 6291460
